TPU v7x, 32 devices: a whole 2x2x4 slice. The times are simulated.
32 devices in a mesh: facet: 8 (over y, x, core), sub: 4 (over z).
Axes of the slice: x: 2, y: 2, z: 4, core: 2. Of those that a mesh axis runs over, the one named last changes fastest.
Arguments:
- model_image: float32 [8, 128, 8192], P('facet'), may hold values from -6 to 6
- step_sizes: float32 [2], replicated, may hold values from 0.3 to 1
- facet_offsets: int32 [2, 8], replicated, may hold values from 0 to 57344
- col_offsets: int32 [4], P('sub'), may hold values from 0 to 65280
- row_offsets: int32 [4, 8], P('sub'), may hold values from 0 to 65280
- counts: int32 [4, 8], P('sub'), may hold values from 1024 to 4096, as said below
- vis_uv: int32 [2, 4, 8, 4096], P(None, 'sub', 'facet'), may hold values from 32 to 2015
- vis_obs: bfloat16 [2, 4, 8, 4096], P(None, 'sub', 'facet'), may hold values from -6 to 6
- vis_weight: bfloat16 [4, 8, 4096], P('sub', 'facet'), may hold values from 0.25 to 4
Outputs:
- updated_image: float32 [8, 128, 8192], P('facet')
- residual_vis: float32 [2, 4, 8, 4096], P(None, 'sub', 'facet')
Inputs may be any that keep to these rules, and one draw needn't show every extreme that they name: The visibilities of a subgrid fill its first counts slots; every draw has a subgrid with exactly 4096 visibilities and one with exactly 1024.
All inputs are finite; a program needn't handle non-finite values.
Results may differ from a plain program's by a relative error of at most 0.017.
Values may be sent and summed in bfloat16 or wider, within the bound.
A program may use at most 64 MiB of HBM per device.

v0:
```python
import math
import jax
import jax.numpy as jnp
from jax import lax
from jax.sharding import PartitionSpec as P

NIMG = 65536
FW = 8192
FROWS = 128
SGW = 256
VCAP = 4096
VB = 512
OS = 8
KSUP = 4
ITERS = 2
two_pi = 2.0 * math.pi


def phase_index(frequency, pixels):
    pixel_low = pixels % 256
    pixel_high = pixels // 256
    return (frequency * pixel_low + frequency * pixel_high % (NIMG // 256) * 256) % NIMG


def row_table(frequency_start, pixel_start):
    frequency = frequency_start + jnp.arange(SGW, dtype=jnp.int32)
    pixels = pixel_start + jnp.arange(FROWS, dtype=jnp.int32)
    angles = phase_index(frequency[:, None], pixels[None, :]).astype(jnp.float32) * (two_pi / NIMG)
    return jnp.concatenate([jnp.cos(angles), jnp.sin(angles)], axis=1).astype(jnp.bfloat16)


def column_table(frequency_start, pixel_start):
    frequency = frequency_start + jnp.arange(SGW, dtype=jnp.int32)
    pixels = pixel_start + jnp.arange(FW, dtype=jnp.int32)
    angles = phase_index(frequency[None, :], pixels[:, None]).astype(jnp.float32) * (two_pi / NIMG)
    return jnp.concatenate([jnp.cos(angles), -jnp.sin(angles)], axis=1).astype(jnp.bfloat16)


def expand_section(section_rows):
    real_half = section_rows[:, :SGW]
    imag_half = section_rows[:, SGW:]
    lower_rows = jnp.concatenate([imag_half, -real_half], axis=1)
    return jnp.concatenate([section_rows, lower_rows], axis=0)


def fold_back(back_rows):
    real_part = back_rows[..., :FROWS, :SGW] - back_rows[..., FROWS:, SGW:]
    imag_part = back_rows[..., :FROWS, SGW:] + back_rows[..., FROWS:, :SGW]
    return jnp.concatenate([real_part, imag_part], axis=-1)


def kernel_rows(position):
    offset = (jnp.arange(SGW, dtype=jnp.int32) * OS + OS // 2)[None, :] - position[:, None]
    distance = offset.astype(jnp.float32) / OS
    inside = jnp.abs(offset) <= KSUP * OS
    return jnp.where(inside, jnp.exp(-0.5 * distance * distance), 0.0).astype(jnp.bfloat16)


def block_pass(grid_bf, row_positions, column_positions, observed, weight, is_live):
    row_kernel = kernel_rows(row_positions)
    column_kernel = kernel_rows(column_positions)
    sampled = jnp.dot(row_kernel, grid_bf, preferred_element_type=jnp.float32)
    column_float = column_kernel.astype(jnp.float32)
    predicted_real = jnp.sum(sampled[:, :SGW] * column_float, axis=1)
    predicted_imag = jnp.sum(sampled[:, SGW:] * column_float, axis=1)
    weight_float = weight.astype(jnp.float32)
    residual_real = jnp.where(
        is_live, weight_float * (observed[0].astype(jnp.float32) - predicted_real), 0.0
    )
    residual_imag = jnp.where(
        is_live, weight_float * (observed[1].astype(jnp.float32) - predicted_imag), 0.0
    )
    weighted = jnp.concatenate(
        [residual_real[:, None] * column_float, residual_imag[:, None] * column_float], axis=1
    ).astype(jnp.bfloat16)
    block_grid = lax.dot_general(
        row_kernel, weighted, (((0,), (0,)), ((), ())), preferred_element_type=jnp.float32
    )
    return (block_grid, jnp.stack([residual_real, residual_imag]))


def sweep_blocks(grid_bf, positions, observed, weight, live_total, blocks):
    length = positions.shape[1]

    def one_block(block_index, running):
        grid_sum, residual = running
        first_row = (block_index * VB).astype(jnp.int32)
        position_part = lax.dynamic_slice_in_dim(positions, first_row, VB, 1)
        observed_part = lax.dynamic_slice_in_dim(observed, first_row, VB, 1)
        weight_part = lax.dynamic_slice_in_dim(weight, first_row, VB, 0)
        is_live = first_row + jnp.arange(VB, dtype=jnp.int32) < live_total
        block_grid, values = block_pass(
            grid_bf, position_part[0], position_part[1], observed_part, weight_part, is_live
        )
        residual = lax.dynamic_update_slice(residual, values, (jnp.int32(0), first_row))
        return (grid_sum + block_grid, residual)

    starting = (jnp.zeros((SGW, 2 * SGW), jnp.float32), jnp.zeros((2, length), jnp.float32))
    return lax.fori_loop(0, blocks, one_block, starting)


def local(
    model_image,
    step_sizes,
    facet_offsets,
    col_offsets,
    row_offsets,
    counts,
    vis_uv,
    vis_obs,
    vis_weight,
):
    facet_count = lax.axis_size("facet")
    norm_factor = 1.0 / math.sqrt(facet_count * FROWS * FW)
    my_facet = lax.axis_index("facet")
    columns_factor = column_table(col_offsets[0], facet_offsets[1, my_facet])
    my_rows = row_offsets[0]
    column_rows = jax.vmap(lambda single: row_table(single, facet_offsets[0, my_facet]))(my_rows)
    facet_rows = jax.vmap(lambda offset: row_table(my_rows[my_facet], offset))(facet_offsets[0])
    own_count = counts[0, my_facet]
    positions = vis_uv[:, 0, 0]
    observed = vis_obs[:, 0, 0]
    weight = vis_weight[0, 0]
    model_now = model_image[0]
    residual = jnp.zeros((2, VCAP), jnp.float32)
    for cycle_index in range(ITERS):
        section_rows = jnp.dot(
            model_now.astype(jnp.bfloat16), columns_factor, preferred_element_type=jnp.float32
        ).astype(jnp.bfloat16)
        pieces = lax.all_gather(section_rows[None], "facet", axis=0, tiled=True)
        expanded_pieces = jax.vmap(expand_section)(pieces)
        summed = lax.dot_general(
            facet_rows,
            expanded_pieces,
            (((0, 2), (0, 1)), ((), ())),
            preferred_element_type=jnp.float32,
        )
        grid_bf = (norm_factor * summed).astype(jnp.bfloat16)
        gridded, residual = sweep_blocks(
            grid_bf, positions, observed, weight, own_count, (own_count + VB - 1) // VB
        )
        gridded_bf = gridded.astype(jnp.bfloat16)
        add_pieces = lax.all_gather(gridded_bf[None], "facet", axis=0, tiled=True)
        add_number = add_pieces.shape[0]
        back_rows = lax.dot_general(
            column_rows.reshape(add_number * SGW, 2 * FROWS),
            add_pieces.reshape(add_number * SGW, 2 * SGW),
            (((0,), (0,)), ((), ())),
            preferred_element_type=jnp.float32,
        )
        adjoint_rows = fold_back(back_rows).astype(jnp.bfloat16)
        partial_gradient = lax.dot_general(
            adjoint_rows,
            columns_factor,
            (((1,), (1,)), ((), ())),
            preferred_element_type=jnp.float32,
        )
        gradient = lax.psum(partial_gradient.astype(jnp.bfloat16), "sub").astype(jnp.float32)
        model_now = model_now + step_sizes[cycle_index] * (norm_factor * gradient)
    return (model_now[None], residual.reshape(2, 1, 1, VCAP))


def solution(mesh):
    in_specs = (
        P("facet", None, None),
        P(),
        P(),
        P("sub"),
        P("sub", None),
        P("sub", None),
        P(None, "sub", "facet", None),
        P(None, "sub", "facet", None),
        P("sub", "facet", None),
    )
    out_specs = (P("facet", None, None), P(None, "sub", "facet", None))
    return jax.shard_map(local, mesh=mesh, in_specs=in_specs, out_specs=out_specs, check_vma=False)
```

profile of v0, /device:TPU:0, one launch (start us, length us, event | category | flops | bytes accessed | tf_op | source)
XLA Modules:
  0.0 421.7 jit_solution(10102998328427896458)
XLA Ops:
  7.2 1.4 constant_dynamic-slice_fusion.4
  10.0 42.6 %cosine_convert_fusion = (bf16[8192,256]{1,0:T(8,128)(2,1)S(1)}, bf16[8192,256]{1,0:T(8,128)(2,1)S(1)}) fusion(s32[8192]{0:T(1024)S(1)} %get-tuple-element.372, s32[8192]{0:T(1024)S(1)} %get-tuple-element.373, s32[256]{0:T(256)S(1)} %iota_add_fusion.3), kind=kLoop, calls=%fused_computation.117 | loop fusion | flops 65011712 | bytes 8455168 | tf_op jit(solution)/shard_map/convert.12
  52.6 1.9 copy-done.2
  54.5 1.4 copy-done.5
  56.0 3.1 fusion.115
  61.9 5.0 %cosine_convert_fusion.1 = (bf16[8,256,128]{2,1,0:T(8,128)(2,1)S(1)}, bf16[8,256,128]{2,1,0:T(8,128)(2,1)S(1)}) fusion(s32[8,128]{1,0:T(8,128)S(1)} %get-tuple-element.369, s32[8,128]{1,0:T(8,128)S(1)} %get-tuple-element.368, s32[256]{0:T(256)S(1)} %iota_add_fusion.4), kind=kLoop, calls=%fused_computation.179 | loop fusion | flops 7864320 | bytes 1057792 | tf_op jit(solution)/shard_map/convert.14
  66.8 18.6 %all-gather.9.cloned.1.call-done = bf16[1024,512]{0,1:T(8,128)(2,1)} async-done(((bf16[128,512]{0,1:T(8,128)(2,1)}), bf16[1024,512]{0,1:T(8,128)(2,1)}) %all-gather.9.cloned.1.call-update) | async-done | bytes 1048592 | tf_op jit(solution)/shard_map/all_gather | solution.py:130
  85.4 1.5 copy.18
  87.8 7.8 %while.30 = (s32[]{:T(128)}, f32[256,512]{1,0:T(8,128)S(1)}, s32[]{:T(128)}, s32[2,4096]{1,0:T(2,128)S(1)}, s32[]{:T(128)}, /*index=5*/bf16[4096]{0:T(1024)(128)...) while((s32[]{:T(128)}, f32[256,512]{1,0:T(8,128)S(1)}, ...), condition=%wide.region_3.4_spmd, body=%wide.region_0.3_spmd.sunk | while | flops 275649536 | bytes 4505811 | solution.py:99
  97.3 5.0 %cosine_convert_fusion.2 = (bf16[8,256,128]{2,1,0:T(8,128)(2,1)S(1)}, bf16[8,256,128]{2,1,0:T(8,128)(2,1)S(1)}) fusion(s32[128]{0:T(128)S(1)} %get-tuple-element.370, s32[128]{0:T(128)S(1)} %get-tuple-element.371, s32[8,256]{1,0:T(8,128)S(1)} %iota_add_fusion.1), kind=kLoop, calls=%fused_computation.181 | loop fusion | flops 7864320 | bytes 1057792 | tf_op jit(solution)/shard_map/convert.16
  102.3 33.9 %all-gather.11.cloned.1.call-done = bf16[2048,512]{1,0:T(8,128)(2,1)} async-done(((bf16[256,512]{1,0:T(8,128)(2,1)}), bf16[2048,512]{1,0:T(8,128)(2,1)}) %all-gather.11.cloned.1.call-update) | async-done | bytes 2097168 | tf_op jit(solution)/shard_map/all_gather | solution.py:143
  136.2 2.5 convolution_bitcast_fusion.1
  139.1 6.4 %convolution_convert_fusion.1 = bf16[128,8192]{1,0:T(8,128)(2,1)} fusion(bf16[128,256]{1,0:T(8,128)(2,1)S(1)} %get-tuple-element.357, bf16[128,256]{1,0:T(8,128)(2,1)S(1)} %get-tuple-element.356, bf16[8192,256]{1,0:T(8,128)(2,1)} %copy-done.5, bf16[8192,256]{1,0:T(8,128)(2,1)S(1)} %copy-done.3), kind=kOutput, calls=%fused_computation.108 | convolution fusion | flops 1091829760 | bytes 10616832 | tf_op jit(solution)/shard_map/dot_general | solution.py:152
  146.8 85.0 %all-reduce.3.cloned.1.call-done = bf16[128,8192]{1,0:T(8,128)(2,1)} async-done(((bf16[128,8192]{1,0:T(8,128)(2,1)}), bf16[128,8192]{1,0:T(8,128)(2,1)}) %all-reduce.3.cloned.1.call-update) | async-done | bytes 2097168 | tf_op jit(solution)/shard_map/psum | solution.py:158
  231.8 7.1 %fusion.111 = bf16[128,512]{1,0:T(8,128)(2,1)} fusion(bf16[128,8192]{1,0:T(8,128)(2,1)} %all-reduce.3.cloned.1.call-done, f32[1,128,8192]{2,1,0:T(8,128)} %param.13, f32[]{:T(128)} %bitcast.23, bf16[8192,256]{1,0:T(8,128)(2,1)} %copy-done.5, bf16[8192,256]{1,0:T(8,128)(2,1)} %copy-done.2), kind=kOutput, calls=%fused_computation.161 | convolution fusion | flops 1094778880 | bytes 14811140 | tf_op jit(solution)/shard_map/dot_general | solution.py:127
  239.0 22.5 %all-gather.13.cloned.1.call-done = bf16[1024,512]{1,0:T(8,128)(2,1)} async-done(((bf16[128,512]{1,0:T(8,128)(2,1)}), bf16[1024,512]{1,0:T(8,128)(2,1)}) %all-gather.13.cloned.1.call-update) | async-done | bytes 1048592 | tf_op jit(solution)/shard_map/all_gather | solution.py:130
  261.5 1.3 fusion.157
  262.8 1.9 fusion.105
  264.8 7.8 %while.31 = (s32[]{:T(128)}, f32[256,512]{1,0:T(8,128)S(1)}, f32[2,4096]{1,0:T(2,128)S(1)}, s32[]{:T(128)}, s32[2,4096]{1,0:T(2,128)S(1)}, /*index=5*/s32[]{:T(1...) while((s32[]{:T(128)}, f32[256,512]{1,0:T(8,128)S(1)}, ...), condition=%wide.region_8.9_spmd, body=%wide.region_5.8_spmd.sunk | while | flops 275650560 | bytes 4514015 | solution.py:99
  273.5 39.9 %all-gather.15.cloned.1.call-done = bf16[2048,512]{1,0:T(8,128)(2,1)} async-done(((bf16[256,512]{1,0:T(8,128)(2,1)}), bf16[2048,512]{1,0:T(8,128)(2,1)}) %all-gather.15.cloned.1.call-update) | async-done | bytes 2097168 | tf_op jit(solution)/shard_map/all_gather | solution.py:143
  313.4 2.5 convolution_bitcast_fusion
  316.2 6.5 %convolution_convert_fusion = bf16[128,8192]{1,0:T(8,128)(2,1)} fusion(bf16[128,256]{1,0:T(8,128)(2,1)S(1)} %get-tuple-element.355, bf16[128,256]{1,0:T(8,128)(2,1)S(1)} %get-tuple-element.354, bf16[8192,256]{1,0:T(8,128)(2,1)} %copy-done.5, bf16[8192,256]{1,0:T(8,128)(2,1)S(1)} %copy-done.4), kind=kOutput, calls=%fused_computation.107 | convolution fusion | flops 1091829760 | bytes 10616832 | tf_op jit(solution)/shard_map/dot_general | solution.py:152
  324.0 85.1 %all-reduce.5.cloned.1.call-done = bf16[128,8192]{1,0:T(8,128)(2,1)} async-done(((bf16[128,8192]{1,0:T(8,128)(2,1)}), bf16[128,8192]{1,0:T(8,128)(2,1)}) %all-reduce.5.cloned.1.call-update) | async-done | bytes 2097168 | tf_op jit(solution)/shard_map/psum | solution.py:158
  409.0 5.8 %add_bitcast_fusion = f32[1,128,8192]{2,1,0:T(8,128)} fusion(bf16[128,8192]{1,0:T(8,128)(2,1)} %all-reduce.5.cloned.1.call-done, bf16[128,8192]{1,0:T(8,128)(2,1)S(1)} %copy-done.6, f32[1,128,8192]{2,1,0:T(8,128)} %param.13, f32[]{:T(128)} %bitcast.28, f32[]{:T(128)} %bitcast.23), kind=kLoop, calls=%fused_computation.120 | loop fusion | flops 6291456 | bytes 12582920 | tf_op jit(solution)/shard_map/broadcast_in_dim | solution.py:160
  (109 shorter events, 23.5 us)
Async XLA Ops:
  7.2 52.0 %copy-start = (s32[1,8]{1,0:T(1,128)S(1)}, s32[1,8]{1,0:T(1,128)}, u32[]{:S(2)}) copy-start(s32[1,8]{1,0:T(1,128)} %param.18) | copy-start | bytes 100
  7.2 78.2 %all-gather.9.cloned.1.call-start = ((), (), s32[]{:S(2)}) async-start(), calls=%async_computation.2 | async-start | bytes 1179648 | tf_op jit(solution)/shard_map/all_gather | solution.py:130
  10.0 46.0 %copy-start.1 = (f32[1,128,8192]{2,1,0:T(8,128)S(1)}, f32[1,128,8192]{2,1,0:T(8,128)}, u32[]{:S(2)}) copy-start(f32[1,128,8192]{2,1,0:T(8,128)} %param.13) | copy-start | bytes 12582916
  52.6 2.0 copy-start.2
  52.6 3.4 copy-start.5
  56.0 4.4 %copy-start.12 = (s32[1,8]{1,0:T(1,128)S(1)}, s32[1,8]{1,0:T(1,128)}, u32[]{:S(2)}) copy-start(s32[1,8]{1,0:T(1,128)} %param.17) | copy-start | bytes 100
  56.0 5.0 %copy-start.8 = (s32[2,1,1,4096]{3,2,1,0:T(1,128)S(1)}, s32[2,1,1,4096]{3,2,1,0:T(1,128)}, u32[]{:S(2)}) copy-start(s32[2,1,1,4096]{3,2,1,0:T(1,128)} %param.19) | copy-start | bytes 98308
  56.0 5.1 %copy-start.9 = (bf16[1,1,4096]{2,1,0:T(2,128)(2,1)S(1)}, bf16[1,1,4096]{2,1,0:T(2,128)(2,1)}, u32[]{:S(2)}) copy-start(bf16[1,1,4096]{2,1,0:T(2,128)(2,1)} %param.21) | copy-start | bytes 24580
  56.0 5.8 %copy-start.11 = (s32[2,8]{1,0:T(2,128)S(1)}, s32[2,8]{1,0:T(2,128)}, u32[]{:S(2)}) copy-start(s32[2,8]{1,0:T(2,128)} %param.15) | copy-start | bytes 196
  59.1 77.2 %all-gather.11.cloned.1.call-start = ((), (), s32[]{:S(2)}) async-start(), calls=%async_computation.3 | async-start | bytes 2359296 | tf_op jit(solution)/shard_map/all_gather | solution.py:143
  87.0 0.8 copy-start.7
  96.3 135.5 %all-reduce.3.cloned.1.call-start = ((), (), s32[]{:S(2)}) async-start(), calls=%async_computation | async-start | bytes 4194304 | tf_op jit(solution)/shard_map/psum | solution.py:158
  136.2 2.8 copy-start.3
  139.1 6.5 %copy-start.10 = (f32[2]{0:T(128)S(1)}, f32[2]{0:T(128)}, u32[]{:S(2)}) copy-start(f32[2]{0:T(128)} %param.14) | copy-start | bytes 28
  145.5 116.0 %all-gather.13.cloned.1.call-start = ((), (), s32[]{:S(2)}) async-start(), calls=%async_computation.4 | async-start | bytes 1179648 | tf_op jit(solution)/shard_map/all_gather | solution.py:130
  239.0 74.4 %all-gather.15.cloned.1.call-start = ((), (), s32[]{:S(2)}) async-start(), calls=%async_computation.5 | async-start | bytes 2359296 | tf_op jit(solution)/shard_map/all_gather | solution.py:143
  273.4 135.6 %all-reduce.5.cloned.1.call-start = ((), (), s32[]{:S(2)}) async-start(), calls=%async_computation.1 | async-start | bytes 4194304 | tf_op jit(solution)/shard_map/psum | solution.py:158
  313.4 2.8 copy-start.4
  316.2 92.8 %copy-start.6 = (bf16[128,8192]{1,0:T(8,128)(2,1)S(1)}, bf16[128,8192]{1,0:T(8,128)(2,1)}, u32[]{:S(2)}) copy-start(bf16[128,8192]{1,0:T(8,128)(2,1)} %all-reduce.3.cloned.1.call-done) | copy-start | bytes 6291460
Sparse Core Ops, SparseCore 0:
  59.2 26.1 all-gather.8
  96.5 39.7 all-gather.10
  145.6 86.1 all-reduce.2
  239.1 22.3 all-gather.12
  273.5 39.8 all-gather.14
  322.9 86.1 all-reduce.4
where the time goes:
time: 422 us
  waiting for transfers between devices  285 us (68%)
  other arithmetic  72.4 us (17%)
  matrix products  36.5 us (9%)
  between operations  16.9 us (4%)
  local copies, waits for them, and re-layouts  10 us (2%)
    psum x2, waiting for transfers between devices, local(): lax.psum(partial_gradient.astype(jnp.bfloat16), 'sub').astype(jnp.float32)  170 us
    all_gather x2, waiting for transfers between devices, local(): add_pieces = lax.all_gather(gridded_bf[None], 'facet', axis=0, tiled=True)  73.8 us
    another operation x11, other arithmetic  54.5 us
    all_gather x2, waiting for transfers between devices, local(): pieces = lax.all_gather(section_rows[None], 'facet', axis=0, tiled=True)  41.1 us
    dot_general x2, matrix products, local(): lax.dot_general(adjoint_rows, columns_factor, (((1,), (1,)), ((), ())), p...  12.9 us
    dot_general x2, matrix products, local(): jnp.dot(model_now.astype(jnp.bfloat16), columns_factor, preferred_element...  10.2 us
  transfers between devices with their start and end apart: 6, of which 6 were waited for; matrix products, arithmetic and copies ran while one was open for 3% of the time, Pallas kernels for 0%

commit v1 on v0

--- a/solution.py
+++ b/solution.py
@@ -14,6 +14,11 @@
 KSUP = 4
 ITERS = 2
 two_pi = 2.0 * math.pi
+
+
+def add_all(block, name):
+    parts = lax.all_gather(block, name)
+    return jnp.sum(parts, axis=0)
 
 
 def phase_index(frequency, pixels):
@@ -155,7 +160,7 @@
             (((1,), (1,)), ((), ())),
             preferred_element_type=jnp.float32,
         )
-        gradient = lax.psum(partial_gradient.astype(jnp.bfloat16), "sub").astype(jnp.float32)
+        gradient = add_all(partial_gradient.astype(jnp.bfloat16), "sub").astype(jnp.float32)
         model_now = model_now + step_sizes[cycle_index] * (norm_factor * gradient)
     return (model_now[None], residual.reshape(2, 1, 1, VCAP))
 

time: 422 us -> 561 us (1.33)
  waiting for transfers between devices: 285 us -> 411 us
  other arithmetic: 72.4 us -> 84.8 us
    all_gather x0 -> x2, waiting for transfers between devices: none -> 297 us  [add_all(): parts = lax.all_gather(block, name)]
    psum x2 -> x0, waiting for transfers between devices: 170 us -> none  [local(): lax.psum(partial_gradient.astype(jnp.bfloat16), 'sub').astype(jnp.float32)]
    reduce_sum x0 -> x2, other arithmetic: none -> 12 us  [add_all(): return jnp.sum(parts, axis=0)]
    add x0 -> x1, other arithmetic: none -> 5.85 us  [local(): model_now = model_now + step_sizes[cycle_index] * (norm_factor * gradient)]
    broadcast_in_dim x1 -> x0, other arithmetic: 5.81 us -> none  [local(): return (model_now[None], residual.reshape(2, 1, 1, VCAP))]
where the time goes in v1:
time: 561 us; the launch traced here: 560 us
  waiting for transfers between devices  411 us (73%)
  other arithmetic  84.8 us (15%)
  matrix products  36.1 us (6%)
  between operations  17.1 us (3%)
  local copies, waits for them, and re-layouts  10.2 us (2%)
    all_gather x2, waiting for transfers between devices, add_all(): parts = lax.all_gather(block, name)  297 us
    all_gather x2, waiting for transfers between devices, local(): add_pieces = lax.all_gather(gridded_bf[None], 'facet', axis=0, tiled=True)  74.2 us
    another operation x11, other arithmetic  54.5 us
    all_gather x2, waiting for transfers between devices, local(): pieces = lax.all_gather(section_rows[None], 'facet', axis=0, tiled=True)  40.1 us
    dot_general x2, matrix products, local(): lax.dot_general(adjoint_rows, columns_factor, (((1,), (1,)), ((), ())), p...  12.7 us
    reduce_sum x2, other arithmetic, add_all(): return jnp.sum(parts, axis=0)  12 us
  transfers between devices with their start and end apart: 6, of which 6 were waited for; matrix products, arithmetic and copies ran while one was open for 3% of the time, Pallas kernels for 0%

profile of v1, /device:TPU:0, one launch (start us, length us, event | category | flops | bytes accessed | tf_op | source)
XLA Modules:
  0.0 560.4 jit_solution(10066084918278083342)
XLA Ops:
  7.2 1.4 constant_dynamic-slice_fusion.4
  10.0 42.6 %cosine_convert_fusion = (bf16[8192,256]{1,0:T(8,128)(2,1)S(1)}, bf16[8192,256]{1,0:T(8,128)(2,1)S(1)}) fusion(s32[8192]{0:T(1024)S(1)} %get-tuple-element.372, s32[8192]{0:T(1024)S(1)} %get-tuple-element.373, s32[256]{0:T(256)S(1)} %iota_add_fusion.3), kind=kLoop, calls=%fused_computation.117 | loop fusion | flops 65011712 | bytes 8455168 | tf_op jit(solution)/shard_map/convert.14
  52.6 2.0 copy-done.2
  56.0 3.0 fusion.115
  62.0 5.0 cosine_convert_fusion.1
  66.9 18.5 %all-gather.13.cloned.1.call-done = bf16[1024,512]{0,1:T(8,128)(2,1)} async-done(((bf16[128,512]{0,1:T(8,128)(2,1)}), bf16[1024,512]{0,1:T(8,128)(2,1)}) %all-gather.13.cloned.1.call-update) | async-done | bytes 1048592 | tf_op jit(solution)/shard_map/all_gather | solution.py:135
  85.4 1.5 copy.18
  87.8 7.9 %while.30 = (s32[]{:T(128)}, f32[256,512]{1,0:T(8,128)S(1)}, s32[]{:T(128)}, s32[2,4096]{1,0:T(2,128)S(1)}, s32[]{:T(128)}, /*index=5*/bf16[4096]{0:T(1024)(128)...) while((s32[]{:T(128)}, f32[256,512]{1,0:T(8,128)S(1)}, ...), condition=%wide.region_3.4_spmd, body=%wide.region_0.3_spmd.sunk | while | flops 275649536 | bytes 4505811 | solution.py:104
  97.5 5.0 cosine_convert_fusion.2
  102.5 34.2 %all-gather.15.cloned.1.call-done = bf16[2048,512]{1,0:T(8,128)(2,1)} async-done(((bf16[256,512]{1,0:T(8,128)(2,1)}), bf16[2048,512]{1,0:T(8,128)(2,1)}) %all-gather.15.cloned.1.call-update) | async-done | bytes 2097168 | tf_op jit(solution)/shard_map/all_gather | solution.py:148
  136.7 2.5 convolution_bitcast_fusion.1
  139.5 6.3 %convolution_convert_fusion.1 = bf16[128,8192]{1,0:T(8,128)(2,1)} fusion(bf16[128,256]{1,0:T(8,128)(2,1)S(1)} %get-tuple-element.357, bf16[128,256]{1,0:T(8,128)(2,1)S(1)} %get-tuple-element.356, bf16[8192,256]{1,0:T(8,128)(2,1)} %copy-done.5, bf16[8192,256]{1,0:T(8,128)(2,1)S(1)} %copy-done.3), kind=kOutput, calls=%fused_computation.108 | convolution fusion | flops 1091829760 | bytes 10616832 | tf_op jit(solution)/shard_map/dot_general | solution.py:157
  147.2 148.4 %all-gather.17.cloned.1.call-done = bf16[512,8192]{1,0:T(8,128)(2,1)} async-done(((bf16[128,8192]{1,0:T(8,128)(2,1)}), bf16[512,8192]{1,0:T(8,128)(2,1)}) %all-gather.17.cloned.1.call-update) | async-done | bytes 8388624 | tf_op jit(solution)/shard_map/all_gather | solution.py:20
  295.6 5.1 reduce_sum.78
  300.8 6.8 %fusion.111 = bf16[128,512]{1,0:T(8,128)(2,1)} fusion(f32[1,128,8192]{2,1,0:T(8,128)} %param.13, bf16[128,8192]{1,0:T(8,128)(2,1)S(1)} %reduce_sum.78, f32[]{:T(128)} %bitcast.24, bf16[8192,256]{1,0:T(8,128)(2,1)} %copy-done.5, bf16[8192,256]{1,0:T(8,128)(2,1)} %copy-done.2), kind=kOutput, calls=%fused_computation.163 | convolution fusion | flops 1094778880 | bytes 14811140 | tf_op jit(solution)/shard_map/dot_general | solution.py:132
  307.6 21.7 %all-gather.19.cloned.1.call-done = bf16[1024,512]{1,0:T(8,128)(2,1)} async-done(((bf16[128,512]{1,0:T(8,128)(2,1)}), bf16[1024,512]{1,0:T(8,128)(2,1)}) %all-gather.19.cloned.1.call-update) | async-done | bytes 1048592 | tf_op jit(solution)/shard_map/all_gather | solution.py:135
  330.5 1.9 fusion.105
  332.6 8.0 %while.31 = (s32[]{:T(128)}, f32[256,512]{1,0:T(8,128)S(1)}, f32[2,4096]{1,0:T(2,128)S(1)}, s32[]{:T(128)}, s32[2,4096]{1,0:T(2,128)S(1)}, /*index=5*/s32[]{:T(1...) while((s32[]{:T(128)}, f32[256,512]{1,0:T(8,128)S(1)}, ...), condition=%wide.region_8.9_spmd, body=%wide.region_5.8_spmd.sunk | while | flops 275650560 | bytes 4514015 | solution.py:104
  341.6 40.0 %all-gather.21.cloned.1.call-done = bf16[2048,512]{1,0:T(8,128)(2,1)} async-done(((bf16[256,512]{1,0:T(8,128)(2,1)}), bf16[2048,512]{1,0:T(8,128)(2,1)}) %all-gather.21.cloned.1.call-update) | async-done | bytes 2097168 | tf_op jit(solution)/shard_map/all_gather | solution.py:148
  381.6 2.6 convolution_bitcast_fusion
  384.6 6.4 %convolution_convert_fusion = bf16[128,8192]{1,0:T(8,128)(2,1)} fusion(bf16[128,256]{1,0:T(8,128)(2,1)S(1)} %get-tuple-element.355, bf16[128,256]{1,0:T(8,128)(2,1)S(1)} %get-tuple-element.354, bf16[8192,256]{1,0:T(8,128)(2,1)} %copy-done.5, bf16[8192,256]{1,0:T(8,128)(2,1)S(1)} %copy-done.4), kind=kOutput, calls=%fused_computation.107 | convolution fusion | flops 1091829760 | bytes 10616832 | tf_op jit(solution)/shard_map/dot_general | solution.py:157
  392.3 148.5 %all-gather.23.cloned.1.call-done = bf16[512,8192]{1,0:T(8,128)(2,1)} async-done(((bf16[128,8192]{1,0:T(8,128)(2,1)}), bf16[512,8192]{1,0:T(8,128)(2,1)}) %all-gather.23.cloned.1.call-update) | async-done | bytes 8388624 | tf_op jit(solution)/shard_map/all_gather | solution.py:20
  540.8 6.9 %reduce_sum.79 = bf16[128,8192]{1,0:T(8,128)(2,1)} reduce(bf16[4,128,8192]{2,1,0:T(8,128)(2,1)} %bitcast.105, bf16[]{:T(256)} %constant.289.clone.1), dimensions={0}, to_apply=%region_9.10 | reduce | flops 3145728 | bytes 10485762 | tf_op jit(solution)/shard_map/reduce_sum | solution.py:21
  547.7 5.9 %bitcast_add_fusion = f32[1,128,8192]{2,1,0:T(8,128)} fusion(f32[1,128,8192]{2,1,0:T(8,128)} %param.13, bf16[128,8192]{1,0:T(8,128)(2,1)} %reduce_sum.79, bf16[128,8192]{1,0:T(8,128)(2,1)S(1)} %reduce_sum.78, f32[]{:T(128)} %bitcast.31, f32[]{:T(128)} %bitcast.24), kind=kLoop, calls=%fused_computation.118 | loop fusion | flops 6291456 | bytes 12582920 | tf_op jit(solution)/shard_map/add | solution.py:164
  (115 shorter events, 26.9 us)
Async XLA Ops:
  7.2 51.9 %copy-start = (s32[1,8]{1,0:T(1,128)S(1)}, s32[1,8]{1,0:T(1,128)}, u32[]{:S(2)}) copy-start(s32[1,8]{1,0:T(1,128)} %param.18) | copy-start | bytes 100
  7.2 78.2 %all-gather.13.cloned.1.call-start = ((), (), s32[]{:S(2)}) async-start(), calls=%async_computation | async-start | bytes 1179648 | tf_op jit(solution)/shard_map/all_gather | solution.py:135
  10.0 46.0 %copy-start.1 = (f32[1,128,8192]{2,1,0:T(8,128)S(1)}, f32[1,128,8192]{2,1,0:T(8,128)}, u32[]{:S(2)}) copy-start(f32[1,128,8192]{2,1,0:T(8,128)} %param.13) | copy-start | bytes 12582916
  52.6 2.0 copy-start.2
  52.6 3.4 copy-start.5
  56.0 4.5 copy-start.14
  56.0 5.2 copy-start.10
  56.0 5.2 copy-start.11
  56.0 5.9 %copy-start.13 = (s32[2,8]{1,0:T(2,128)S(1)}, s32[2,8]{1,0:T(2,128)}, u32[]{:S(2)}) copy-start(s32[2,8]{1,0:T(2,128)} %param.15) | copy-start | bytes 196
  59.0 77.6 %all-gather.15.cloned.1.call-start = ((), (), s32[]{:S(2)}) async-start(), calls=%async_computation.1 | async-start | bytes 2359296 | tf_op jit(solution)/shard_map/all_gather | solution.py:148
  87.0 0.8 copy-start.9
  96.5 199.1 %all-gather.17.cloned.1.call-start = ((), (), s32[]{:S(2)}) async-start(), calls=%async_computation.2 | async-start | bytes 10485760 | tf_op jit(solution)/shard_map/all_gather | solution.py:20
  102.5 43.4 %copy-start.6 = (bf16[8,256,128]{2,1,0:T(8,128)(2,1)}, bf16[8,256,128]{2,1,0:T(8,128)(2,1)S(1)}, u32[]{:S(2)}) copy-start(bf16[8,256,128]{2,1,0:T(8,128)(2,1)S(1)} %get-tuple-element.360) | copy-start | bytes 1572868
  102.5 43.3 %copy-start.8 = (bf16[8,256,128]{2,1,0:T(8,128)(2,1)}, bf16[8,256,128]{2,1,0:T(8,128)(2,1)S(1)}, u32[]{:S(2)}) copy-start(bf16[8,256,128]{2,1,0:T(8,128)(2,1)S(1)} %get-tuple-element.361) | copy-start | bytes 1572868
  136.7 2.8 copy-start.3
  139.5 6.4 %copy-start.12 = (f32[2]{0:T(128)S(1)}, f32[2]{0:T(128)}, u32[]{:S(2)}) copy-start(f32[2]{0:T(128)} %param.14) | copy-start | bytes 28
  145.9 183.4 %all-gather.19.cloned.1.call-start = ((), (), s32[]{:S(2)}) async-start(), calls=%async_computation.3 | async-start | bytes 1179648 | tf_op jit(solution)/shard_map/all_gather | solution.py:135
  307.6 74.0 %all-gather.21.cloned.1.call-start = ((), (), s32[]{:S(2)}) async-start(), calls=%async_computation.4 | async-start | bytes 2359296 | tf_op jit(solution)/shard_map/all_gather | solution.py:148
  332.6 49.1 %copy-start.7 = (bf16[8,256,128]{2,1,0:T(8,128)(2,1)S(1)}, bf16[8,256,128]{2,1,0:T(8,128)(2,1)}, u32[]{:S(2)}) copy-start(bf16[8,256,128]{2,1,0:T(8,128)(2,1)} %copy-done.6) | copy-start | bytes 1572868
  341.3 199.4 %all-gather.23.cloned.1.call-start = ((), (), s32[]{:S(2)}) async-start(), calls=%async_computation.5 | async-start | bytes 10485760 | tf_op jit(solution)/shard_map/all_gather | solution.py:20
  381.6 3.0 copy-start.4
Sparse Core Ops, SparseCore 0:
  59.2 26.1 all-gather.12
  96.6 40.0 all-gather.14
  146.0 149.6 all-gather.16
  307.7 21.5 all-gather.18
  341.5 40.1 all-gather.20
  391.1 149.5 all-gather.22
